TPU v7x, 32 devices: a whole 2x2x4 slice. The times are simulated.
32 devices in a mesh: cp: 16 (over z, x, core), tp: 2 (over y).
Axes of the slice: x: 2, y: 2, z: 4, core: 2. Of those that a mesh axis runs over, the one named last changes fastest.
Arguments:
- hidden: bfloat16 [8192, 4096], P('cp', 'tp'), may hold values from -6 to 6
- norm_gain: float32 [4096], replicated, may hold values from 0.5 to 1.5
- w_query: bfloat16 [4096, 4096], P(None, 'tp'), may hold values from -0.140625 to 0.140625
- w_key: bfloat16 [4096, 1024], P(None, 'tp'), may hold values from -4 to 4
- w_value: bfloat16 [4096, 1024], P(None, 'tp'), may hold values from -0.09375 to 0.09375
- w_out: bfloat16 [4096, 4096], P('tp'), may hold values from -0.5 to 0.5
- doc_ids: int32 [8192], P('cp'), may hold values from 0 to 5, never falling along the last dimension, each value on 1 to 6144 neighbouring positions
Outputs:
- updated: bfloat16 [8192, 4096], P('cp', 'tp')
Inputs may be any that keep to these rules, and one draw needn't show every extreme that they name: `doc_ids`: document numbers never fall along the sequence; every document has 1 to 6144 tokens.
All inputs are finite; a program needn't handle non-finite values.
Results may differ from a plain program's by a relative error of at most 0.017.
The roundings to bfloat16 on the way count: a program that leaves them out, or rounds other values in their place, can miss the bound.
Values may be sent and summed in bfloat16 or wider, within the bound.
A program may use at most 128 MiB of HBM per device.

v0:
```python
import jax
import jax.numpy as jnp
from jax import lax
from jax.sharding import PartitionSpec as P

HEADS = 32
KV_HEADS = 8
HEAD_SIZE = 128
epsilon = 1e-05
rope_base = 500000.0


def rotate(vectors, positions):
    half = HEAD_SIZE // 2
    freqs = rope_base ** (-jnp.arange(half, dtype=jnp.float32) * 2.0 / HEAD_SIZE)
    angles = positions.astype(jnp.float32)[:, None] * freqs[None, :]
    cosine = jnp.cos(angles)[:, None, :]
    sine = jnp.sin(angles)[:, None, :]
    first = vectors[..., :half]
    second = vectors[..., half:]
    return jnp.concatenate(
        [first * cosine - second * sine, second * cosine + first * sine], axis=-1
    )


def attend_block(
    loop_state, query_matrix, query_pos, query_doc, key_matrix, value_matrix, key_pos, key_doc
):
    best, total, running_output = loop_state
    logit_matrix = jnp.einsum(
        "ucpm,ycm->cpuy", query_matrix, key_matrix, preferred_element_type=jnp.float32
    ) * HEAD_SIZE ** (-0.5)
    allowed = (key_pos[None, :] <= query_pos[:, None]) & (key_doc[None, :] == query_doc[:, None])
    masked = jnp.where(allowed, logit_matrix, jnp.float32(-1e30))
    new_best = jnp.maximum(best, jnp.max(masked, axis=-1))
    correction_scale = jnp.exp(best - new_best)
    attention_weights = jnp.where(
        allowed, jnp.exp(logit_matrix - new_best[..., None]), jnp.float32(0.0)
    )
    total = total * correction_scale + jnp.sum(attention_weights, axis=-1)
    running_output = running_output * correction_scale[..., None] + jnp.einsum(
        "sfec,csh->sfeh",
        attention_weights.astype(jnp.bfloat16),
        value_matrix,
        preferred_element_type=jnp.float32,
    )
    return (new_best, total, running_output)


def shards(hidden, norm_gain, w_query, w_key, w_value, w_out, doc_ids):
    tok_rows = hidden.shape[0]
    half_rows = tok_rows // 2
    width = norm_gain.shape[0]
    group = HEADS // KV_HEADS
    local_kv = w_key.shape[1] // HEAD_SIZE
    query_cols = w_query.shape[1]
    key_cols = w_key.shape[1]
    wide_local = hidden.astype(jnp.float32)
    squares = lax.psum(jnp.sum(wide_local * wide_local, axis=1), "tp")
    inverse_rms = lax.rsqrt(squares / width + epsilon)[:, None]
    piece = lax.all_gather(hidden, "tp", axis=1, tiled=True)
    normed_piece = (piece.astype(jnp.float32) * inverse_rms * norm_gain[None, :]).astype(
        jnp.bfloat16
    )
    projected = jnp.concatenate(
        [
            jnp.dot(normed_piece, w_query, preferred_element_type=jnp.float32),
            jnp.dot(normed_piece, w_key, preferred_element_type=jnp.float32),
            jnp.dot(normed_piece, w_value, preferred_element_type=jnp.float32),
        ],
        axis=1,
    )
    cp_rank = lax.axis_index("cp")
    positions = cp_rank * tok_rows + jnp.arange(tok_rows, dtype=jnp.int32)
    query_raw = projected[:, :query_cols].reshape(tok_rows, local_kv * group, HEAD_SIZE)
    key_raw = projected[:, query_cols : query_cols + key_cols].reshape(
        tok_rows, local_kv, HEAD_SIZE
    )
    query_matrix = (
        rotate(query_raw, positions)
        .astype(jnp.bfloat16)
        .reshape(tok_rows, local_kv, group, HEAD_SIZE)
    )
    keys_flat = rotate(key_raw, positions).astype(jnp.bfloat16).reshape(tok_rows, key_cols)
    values_flat = projected[:, query_cols + key_cols :].astype(jnp.bfloat16)
    query_doc = doc_ids.astype(jnp.float32)
    docs_flat = query_doc.astype(jnp.bfloat16)
    first_queries = query_matrix[:half_rows]
    first_pos = positions[:half_rows]
    first_doc = query_doc[:half_rows]
    second_queries = query_matrix[half_rows:]
    second_doc = query_doc[half_rows:]
    second_start = cp_rank * tok_rows + half_rows
    second_pos = second_start + jnp.arange(half_rows, dtype=jnp.int32)
    last_first = cp_rank * tok_rows + half_rows - 1
    last_second = second_start + half_rows - 1
    init_half = (
        jnp.full((local_kv, group, half_rows), -1e30, jnp.float32),
        jnp.zeros((local_kv, group, half_rows), jnp.float32),
        jnp.zeros((local_kv, group, half_rows, HEAD_SIZE), jnp.float32),
    )
    init = (init_half, init_half)
    key_piece = lax.all_gather(keys_flat, "cp", axis=0, tiled=True)
    value_piece = lax.all_gather(values_flat, "cp", axis=0, tiled=True)
    doc_piece = lax.all_gather(docs_flat, "cp", axis=0, tiled=True)
    count = key_piece.shape[0]

    def inner(index, state):
        first_state, second_state = state
        offset = index * tok_rows
        key_blk = lax.dynamic_slice_in_dim(key_piece, offset, tok_rows, 0).reshape(
            tok_rows, local_kv, HEAD_SIZE
        )
        value_blk = lax.dynamic_slice_in_dim(value_piece, offset, tok_rows, 0).reshape(
            tok_rows, local_kv, HEAD_SIZE
        )
        key_doc = lax.dynamic_slice_in_dim(doc_piece, offset, tok_rows, 0).astype(jnp.float32)
        key_pos = offset + jnp.arange(tok_rows, dtype=jnp.int32)

        def attend_first(inner_state):
            return attend_block(
                inner_state,
                first_queries,
                first_pos,
                first_doc,
                key_blk,
                value_blk,
                key_pos,
                key_doc,
            )

        def attend_second(inner_state):
            return attend_block(
                inner_state,
                second_queries,
                second_pos,
                second_doc,
                key_blk,
                value_blk,
                key_pos,
                key_doc,
            )

        first_state = lax.cond(
            offset <= last_first, attend_first, lambda inner_state: inner_state, first_state
        )
        second_state = lax.cond(
            offset <= last_second, attend_second, lambda inner_state: inner_state, second_state
        )
        return (first_state, second_state)

    final = lax.fori_loop(0, count // tok_rows, inner, init)

    def finish(state):
        result = state[2] / state[1][..., None]
        return (
            jnp.transpose(result, (2, 0, 1, 3)).reshape(half_rows, query_cols).astype(jnp.bfloat16)
        )

    attended_first = finish(final[0])
    attended_second = finish(final[1])
    attended = jnp.concatenate([attended_first, attended_second], axis=0)
    terms = jnp.dot(attended, w_out, preferred_element_type=jnp.float32)
    summed = lax.psum_scatter(terms.astype(jnp.bfloat16), "tp", scatter_dimension=1, tiled=True)
    return summed


def solution(mesh):
    in_specs = (
        P("cp", "tp"),
        P(),
        P(None, "tp"),
        P(None, "tp"),
        P(None, "tp"),
        P("tp", None),
        P("cp"),
    )
    out_specs = P("cp", "tp")
    return jax.shard_map(shards, mesh=mesh, in_specs=in_specs, out_specs=out_specs, check_vma=False)
```

profile of v0, /device:TPU:0, one launch (start us, length us, event | category | flops | bytes accessed | tf_op | source)
XLA Modules:
  0.0 622.3 jit_solution(9094426565222155319)
XLA Ops:
  7.3 2.1 multiply_reduce_fusion
  9.4 5.9 psum.7
  15.8 52.5 %all-gather.5.cloned.1.call-done = bf16[512,4096]{1,0:T(8,128)(2,1)} async-done(((bf16[512,2048]{1,0:T(8,128)(2,1)}), bf16[512,4096]{1,0:T(8,128)(2,1)}) %all-gather.5.cloned.1.call-update) | async-done | bytes 4194320 | tf_op jit(solution)/shard_map/all_gather | solution.py:61
  68.4 5.9 fusion.44
  75.4 6.6 %convolution_convert_fusion.1 = bf16[512,512]{1,0:T(8,128)(2,1)} fusion(bf16[4096,512]{1,0:T(8,128)(2,1)} %param.17, bf16[512,4096]{1,0:T(8,128)(2,1)} %all-gather.5.cloned.1.call-done, f32[4096]{0:T(1024)S(1)} %copy-done.7, f32[512]{0:T(512)S(1)} %add_rsqrt_fusion), kind=kOutput, calls=%fused_computation.61 | convolution fusion | flops 2156134400 | bytes 8931328 | tf_op jit(solution)/shard_map/dot_general | solution.py:69
  82.4 22.4 %all-gather = bf16[16,1,512]{2,1,0:T(2,128)(2,1)S(1)} all-gather(bf16[1,1,512]{2,1,0:T(2,128)(2,1)S(1)} %reshape.106), channel_id=1, replica_groups=mesh['cp'=16,'tp'=2] {'cp'}, dimensions={0}, use_global_device_ids=true | all-gather | bytes 17408 | tf_op jit(solution)/shard_map/all_gather | solution.py:105
  105.0 13.1 %convolution_bitcast_fusion = f32[64,8,16,128]{3,1,2,0:T(8,128)S(1)} fusion(bf16[4096,2048]{1,0:T(8,128)(2,1)} %param.15, bf16[512,4096]{1,0:T(8,128)(2,1)} %all-gather.5.cloned.1.call-done, f32[4096]{0:T(1024)S(1)} %copy-done.7, f32[512]{0:T(512)S(1)} %add_rsqrt_fusion), kind=kOutput, calls=%fused_computation.53 | convolution fusion | flops 8598323200 | bytes 25184256 | tf_op jit(solution)/shard_map/dot_general | solution.py:67
  119.0 1.6 add_convert_fusion
  122.3 31.2 %all-gather.7.cloned.1.call-done = bf16[8192,512]{0,1:T(8,128)(2,1)} async-done(((bf16[512,512]{0,1:T(8,128)(2,1)}), bf16[8192,512]{0,1:T(8,128)(2,1)}) %all-gather.7.cloned.1.call-update) | async-done | bytes 8388624 | tf_op jit(solution)/shard_map/all_gather | solution.py:103
  153.5 74.7 %all-gather.9.cloned.1.call-done = bf16[8192,512]{1,0:T(8,128)(2,1)} async-done(((bf16[512,512]{1,0:T(8,128)(2,1)}), bf16[8192,512]{1,0:T(8,128)(2,1)}) %all-gather.9.cloned.1.call-update) | async-done | bytes 8388624 | tf_op jit(solution)/shard_map/all_gather | solution.py:104
  229.7 1.6 broadcast_in_dim.42.clone
  231.3 68.3 %while.24 = (s32[]{:T(128)}, f32[4,4,256]{2,1,0:T(4,128)S(1)}, f32[4,4,256]{2,1,0:T(4,128)S(1)}, f32[4,4,256,128]{3,2,1,0:T(8,128)}, f32[4,4,256]{2,1,0:T(4,128)...) while((s32[]{:T(128)}, f32[4,4,256]{2,1,0:T(4,128)S(1)}, ...), condition=%wide.region_11.12_spmd.clone, body=%wide.region_2.11_spmd.clone.sunk | while | flops 2196522240 | bytes 105403112 | solution.py:152
  234.5 8.1 %conditional.6 = ((f32[4,4,256]{2,1,0:T(4,128)S(1)}, f32[4,4,256]{2,1,0:T(4,128)S(1)}, f32[4,4,256,128]{3,2,1,0:T(8,128)})) conditional(s32[]{:T(128)} %convert_element_type.128, (f32[4,4,256]{2,1,0:T(4,128)S(1)}, f32[4,4,256]{2,1,0:T(4,128)S(1)}, f32[4,4,256,128]{3,2,1,0:T(8,128)}) %tuple.72, (s32[512]{0:T(512)S(1)}, s32[256]{0:T(256)S(1)}, ...), branch_computations={%region_3.0_spmd, %region_4.6_spmd} | conditional | flops 1098260480 | bytes 51124340 | solution.py:144
  236.3 1.7 fusion.6
  238.1 3.2 multiply_add_fusion
  242.6 8.1 %conditional.7 = ((f32[4,4,256]{2,1,0:T(4,128)S(1)}, f32[4,4,256]{2,1,0:T(4,128)S(1)}, f32[4,4,256,128]{3,2,1,0:T(8,128)})) conditional(s32[]{:T(128)} %convert_element_type.129, (f32[4,4,256]{2,1,0:T(4,128)S(1)}, f32[4,4,256]{2,1,0:T(4,128)S(1)}, f32[4,4,256,128]{3,2,1,0:T(8,128)}) %tuple.74, (s32[512]{0:T(512)S(1)}, s32[]{:T(128)}, ...), branch_computations={%region_7.7_spmd, %region_8.10_spmd} | conditional | flops 1098260736 | bytes 51126392 | solution.py:147
  242.8 1.6 fusion.20
  244.4 1.7 fusion.24
  246.1 3.2 multiply_add_fusion.2
  299.6 1.9 copy.40
  301.5 2.9 copy.39
  304.4 2.1 divide_convert_fusion
  306.5 14.0 %convolution_convert_fusion = bf16[512,4096]{1,0:T(8,128)(2,1)} fusion(bf16[2048,4096]{1,0:T(8,128)(2,1)} %param.18, bf16[256,2048]{0,1:T(8,128)(2,1)S(1)} %bitcast.110, bf16[256,2048]{0,1:T(8,128)(2,1)S(1)} %bitcast.111), kind=kOutput, calls=%fused_computation.49 | convolution fusion | flops 8596226048 | bytes 23068672 | tf_op jit(solution)/shard_map/dot_general | solution.py:163
  320.5 295.2 %reduce-scatter.2.cloned.1.call-done = bf16[512,2048]{1,0:T(8,128)(2,1)} async-done(((bf16[512,4096]{1,0:T(8,128)(2,1)}), bf16[512,2048]{1,0:T(8,128)(2,1)}) %reduce-scatter.2.cloned.1.call-update) | async-done | bytes 2097168 | tf_op jit(solution)/shard_map/reduce_scatter | solution.py:164
  (184 shorter events, 63.7 us)
Async XLA Ops:
  6.5 61.8 %copy-start.7 = (f32[4096]{0:T(1024)S(1)}, f32[4096]{0:T(1024)}, u32[]{:S(2)}) copy-start(f32[4096]{0:T(1024)} %param.14) | copy-start | bytes 49156
  6.5 61.8 %all-gather.5.cloned.1.call-start = ((), (), s32[]{:S(2)}) async-start(), calls=%async_computation.1 | async-start | bytes 6291456 | tf_op jit(solution)/shard_map/all_gather | solution.py:61
  7.3 146.2 %all-gather.7.cloned.1.call-start = ((), (), s32[]{:S(2)}) async-start(), calls=%async_computation.2 | async-start | bytes 8912896 | tf_op jit(solution)/shard_map/all_gather | solution.py:103
  75.3 7.0 %copy-start.6 = (s32[512]{0:T(512)S(1)}, s32[512]{0:T(512)}, u32[]{:S(2)}) copy-start(s32[512]{0:T(512)} %param.19) | copy-start | bytes 6148
  75.4 152.8 %all-gather.9.cloned.1.call-start = ((), (), s32[]{:S(2)}) async-start(), calls=%async_computation.3 | async-start | bytes 8912896 | tf_op jit(solution)/shard_map/all_gather | solution.py:104
  82.1 533.7 %reduce-scatter.2.cloned.1.call-start = ((), (), s32[]{:S(2)}) async-start(), calls=%async_computation.4 | async-start | bytes 6291456 | tf_op jit(solution)/shard_map/reduce_scatter | solution.py:164
  236.3 1.8 copy-start
  236.3 1.8 copy-start.2
  241.2 1.3 copy-start.3
  244.4 1.8 copy-start.1
  244.4 1.8 copy-start.4
  249.3 1.3 copy-start.5
Sparse Core Ops, SparseCore 0:
  8.9 59.4 all-gather.4
  75.5 77.9 all-gather.6
  155.6 72.4 all-gather.8
  320.7 295.0 reduce-scatter.1
where the time goes:
time: 625 us; the launch traced here: 622 us
  waiting for transfers between devices  454 us (73%)
  local copies, waits for them, and re-layouts  63.1 us (10%)
  matrix products  49.1 us (8%)
  blocking collectives  28.3 us (5%)
  other arithmetic  13.6 us (2%)
  between operations  13.3 us (2%)
    reduce_scatter x1, waiting for transfers between devices, shards(): lax.psum_scatter(terms.astype(jnp.bfloat16), 'tp', scatter_dimension=1, t...  295 us
    all_gather x1, waiting for transfers between devices, shards(): value_piece = lax.all_gather(values_flat, 'cp', axis=0, tiled=True)  74.7 us
    all_gather x1, waiting for transfers between devices, shards(): piece = lax.all_gather(hidden, 'tp', axis=1, tiled=True)  52.5 us
    dynamic_slice x32, local copies, waits for them, and re-layouts, inner(): lax.dynamic_slice_in_dim(value_piece, offset, tok_rows, 0)  33.5 us
    all_gather x1, waiting for transfers between devices, shards(): key_piece = lax.all_gather(keys_flat, 'cp', axis=0, tiled=True)  31.2 us
    all_gather x1, blocking collectives, shards(): doc_piece = lax.all_gather(docs_flat, 'cp', axis=0, tiled=True)  22.4 us
    dynamic_slice x16, local copies, waits for them, and re-layouts, inner(): lax.dynamic_slice_in_dim(key_piece, offset, tok_rows, 0)  17.2 us
    dot_general x1, matrix products, shards(): terms = jnp.dot(attended, w_out, preferred_element_type=jnp.float32)  14 us
  transfers between devices with their start and end apart: 4, of which 4 were waited for; matrix products, arithmetic and copies ran while one was open for 4% of the time, Pallas kernels for 0%

commit v1 on v0

--- a/solution.py
+++ b/solution.py
@@ -100,8 +100,11 @@
         jnp.zeros((local_kv, group, half_rows, HEAD_SIZE), jnp.float32),
     )
     init = (init_half, init_half)
-    key_piece = lax.all_gather(keys_flat, "cp", axis=0, tiled=True)
-    value_piece = lax.all_gather(values_flat, "cp", axis=0, tiled=True)
+    key_piece, value_piece = jnp.split(
+        lax.all_gather(jnp.concatenate([keys_flat, values_flat], axis=1), "cp", axis=0, tiled=True),
+        [keys_flat.shape[1]],
+        axis=1,
+    )
     doc_piece = lax.all_gather(docs_flat, "cp", axis=0, tiled=True)
     count = key_piece.shape[0]
 

time: 625 us -> 583 us (0.933)
  local copies, waits for them, and re-layouts: 63.1 us -> 44.3 us
  waiting for transfers between devices: 454 us -> 436 us
    dynamic_slice x16 -> x0, local copies, waits for them, and re-layouts: 17.2 us -> none  [inner(): lax.dynamic_slice_in_dim(key_piece, offset, tok_rows, 0)]
    all_gather x2 -> x1, waiting for transfers between devices: 106 us -> 90.2 us  [shards(): lax.all_gather(jnp.concatenate([keys_flat, values_flat], axis=1), 'cp', a...]
    dynamic_slice x32 -> x16, local copies, waits for them, and re-layouts: 33.5 us -> 20.4 us  [inner(): lax.dynamic_slice_in_dim(value_piece, offset, tok_rows, 0)]
    split x0 -> x1, local copies, waits for them, and re-layouts: none -> 11.5 us  [shards(): jnp.split(lax.all_gather(jnp.concatenate([keys_flat, values_flat], axis=1...]
  transfers between devices with their start and end apart: 4 -> 3, of which waited for: 4 -> 3; matrix products, arithmetic and copies ran while one was open for 4% -> 3% of each run, Pallas kernels for 0% -> 0%
where the time goes in v1:
time: 583 us
  waiting for transfers between devices  436 us (75%)
  matrix products  45.3 us (8%)
  local copies, waits for them, and re-layouts  44.3 us (8%)
  blocking collectives  28 us (5%)
  other arithmetic  14 us (2%)
  between operations  13.3 us (2%)
    reduce_scatter x1, waiting for transfers between devices, shards(): lax.psum_scatter(terms.astype(jnp.bfloat16), 'tp', scatter_dimension=1, t...  293 us
    all_gather x1, waiting for transfers between devices, shards(): lax.all_gather(jnp.concatenate([keys_flat, values_flat], axis=1), 'cp', a...  90.2 us
    all_gather x1, waiting for transfers between devices, shards(): piece = lax.all_gather(hidden, 'tp', axis=1, tiled=True)  52.5 us
    all_gather x1, blocking collectives, shards(): doc_piece = lax.all_gather(docs_flat, 'cp', axis=0, tiled=True)  22.1 us
    dynamic_slice x16, local copies, waits for them, and re-layouts, inner(): lax.dynamic_slice_in_dim(value_piece, offset, tok_rows, 0)  20.4 us
    dot_general x1, matrix products, shards(): terms = jnp.dot(attended, w_out, preferred_element_type=jnp.float32)  14 us
    dot_general x1, matrix products, shards(): jnp.dot(normed_piece, w_query, preferred_element_type=jnp.float32)  13.1 us
  transfers between devices with their start and end apart: 3, of which 3 were waited for; matrix products, arithmetic and copies ran while one was open for 3% of the time, Pallas kernels for 0%

profile of v1, /device:TPU:0, one launch (start us, length us, event | category | flops | bytes accessed | tf_op | source)
XLA Modules:
  0.0 582.8 jit_solution(12041520822038819065)
XLA Ops:
  7.3 2.1 multiply_reduce_fusion
  9.4 5.9 %psum.7 = f32[512]{0:T(512)S(1)} all-reduce(f32[512]{0:T(512)S(1)} %multiply_reduce_fusion), channel_id=1, replica_groups=mesh['cp'=16,'tp'=2] {'tp'}, use_global_device_ids=true, to_apply=%region_1.0 | all-reduce | flops 512 | bytes 4096 | tf_op jit(solution)/shard_map/psum | solution.py:59
  15.8 52.5 %all-gather.4.cloned.1.call-done = bf16[512,4096]{1,0:T(8,128)(2,1)} async-done(((bf16[512,2048]{1,0:T(8,128)(2,1)}), bf16[512,4096]{1,0:T(8,128)(2,1)}) %all-gather.4.cloned.1.call-update) | async-done | bytes 4194320 | tf_op jit(solution)/shard_map/all_gather | solution.py:61
  68.4 6.1 %fusion.44 = f32[512,512]{0,1:T(8,128)S(1)} fusion(bf16[4096,512]{1,0:T(8,128)(2,1)} %param.16, bf16[512,4096]{1,0:T(8,128)(2,1)} %all-gather.4.cloned.1.call-done, f32[4096]{0:T(1024)S(1)} %copy-done.7, f32[512]{0:T(512)S(1)} %add_rsqrt_fusion), kind=kOutput, calls=%fused_computation.76 | convolution fusion | flops 2155872256 | bytes 9455616 | tf_op jit(solution)/shard_map/dot_general | solution.py:68
  74.7 2.6 convolution_convert_fusion.1
  78.7 22.1 %all-gather = bf16[16,1,512]{2,1,0:T(2,128)(2,1)S(1)} all-gather(bf16[1,1,512]{2,1,0:T(2,128)(2,1)S(1)} %reshape.106), channel_id=1, replica_groups=mesh['cp'=16,'tp'=2] {'cp'}, dimensions={0}, use_global_device_ids=true | all-gather | bytes 17408 | tf_op jit(solution)/shard_map/all_gather | solution.py:108
  101.0 13.1 %convolution_bitcast_fusion = f32[64,8,16,128]{3,1,2,0:T(8,128)S(1)} fusion(bf16[4096,2048]{1,0:T(8,128)(2,1)} %param.15, bf16[512,4096]{1,0:T(8,128)(2,1)} %all-gather.4.cloned.1.call-done, f32[4096]{0:T(1024)S(1)} %copy-done.7, f32[512]{0:T(512)S(1)} %add_rsqrt_fusion), kind=kOutput, calls=%fused_computation.53 | convolution fusion | flops 8598323200 | bytes 25184256 | tf_op jit(solution)/shard_map/dot_general | solution.py:67
  115.0 1.6 add_convert_fusion
  118.3 90.2 %all-gather.6.cloned.1.call-done = bf16[8192,1024]{0,1:T(8,128)(2,1)} async-done(((bf16[512,1024]{0,1:T(8,128)(2,1)}), bf16[8192,1024]{0,1:T(8,128)(2,1)}) %all-gather.6.cloned.1.call-update) | async-done | bytes 16777232 | tf_op jit(solution)/shard_map/all_gather | solution.py:104
  208.5 11.5 %fusion.45 = (bf16[8192,512]{0,1:T(8,128)(2,1)}, bf16[8192,512]{0,1:T(8,128)(2,1)}) fusion(bf16[8192,1024]{0,1:T(8,128)(2,1)} %all-gather.6.cloned.1.call-done), kind=kLoop, calls=%fused_computation.77 | loop fusion | bytes 33554432 | tf_op jit(solution)/shard_map/split | solution.py:103
  223.2 39.6 %while.24 = (s32[]{:T(128)}, f32[4,4,256]{2,1,0:T(4,128)S(1)}, f32[4,4,256]{2,1,0:T(4,128)S(1)}, f32[4,4,256,128]{3,2,1,0:T(8,128)}, f32[4,4,256]{2,1,0:T(4,128)...) while((s32[]{:T(128)}, f32[4,4,256]{2,1,0:T(4,128)S(1)}, ...), condition=%wide.region_11.12_spmd.clone, body=%wide.region_2.11_spmd.clone.sunk | while | flops 2196522240 | bytes 100160168 | solution.py:155
  224.5 8.1 %conditional.7 = ((f32[4,4,256]{2,1,0:T(4,128)S(1)}, f32[4,4,256]{2,1,0:T(4,128)S(1)}, f32[4,4,256,128]{3,2,1,0:T(8,128)})) conditional(s32[]{:T(128)} %convert_element_type.129, (f32[4,4,256]{2,1,0:T(4,128)S(1)}, f32[4,4,256]{2,1,0:T(4,128)S(1)}, f32[4,4,256,128]{3,2,1,0:T(8,128)}) %tuple.77, (s32[512]{0:T(512)S(1)}, s32[]{:T(128)}, ...), branch_computations={%region_7.7_spmd, %region_8.10_spmd} | conditional | flops 1098260736 | bytes 49029212 | solution.py:150
  224.8 1.5 fusion.20
  226.4 1.7 fusion.24
  228.1 3.2 multiply_add_fusion.2
  232.6 8.0 %conditional.6 = ((f32[4,4,256]{2,1,0:T(4,128)S(1)}, f32[4,4,256]{2,1,0:T(4,128)S(1)}, f32[4,4,256,128]{3,2,1,0:T(8,128)})) conditional(s32[]{:T(128)} %convert_element_type.128, (f32[4,4,256]{2,1,0:T(4,128)S(1)}, f32[4,4,256]{2,1,0:T(4,128)S(1)}, f32[4,4,256,128]{3,2,1,0:T(8,128)}) %tuple.75, (s32[512]{0:T(512)S(1)}, s32[256]{0:T(256)S(1)}, ...), branch_computations={%region_3.0_spmd, %region_4.6_spmd} | conditional | flops 1098260480 | bytes 49027160 | solution.py:147
  232.8 1.6 fusion.2
  234.4 1.7 fusion.6
  236.1 3.2 multiply_add_fusion
  262.8 1.9 copy.39
  264.7 2.9 copy.38
  267.6 2.1 divide_convert_fusion
  269.7 14.0 %convolution_convert_fusion = bf16[512,4096]{1,0:T(8,128)(2,1)} fusion(bf16[2048,4096]{1,0:T(8,128)(2,1)} %param.18, bf16[256,2048]{0,1:T(8,128)(2,1)S(1)} %bitcast.110, bf16[256,2048]{0,1:T(8,128)(2,1)S(1)} %bitcast.111), kind=kOutput, calls=%fused_computation.49 | convolution fusion | flops 8596226048 | bytes 23068672 | tf_op jit(solution)/shard_map/dot_general | solution.py:166
  283.7 292.5 %reduce-scatter.2.cloned.1.call-done = bf16[512,2048]{1,0:T(8,128)(2,1)} async-done(((bf16[512,4096]{1,0:T(8,128)(2,1)}), bf16[512,2048]{1,0:T(8,128)(2,1)}) %reduce-scatter.2.cloned.1.call-update) | async-done | bytes 2097168 | tf_op jit(solution)/shard_map/reduce_scatter | solution.py:167
  (151 shorter events, 34.1 us)
Async XLA Ops:
  6.5 61.8 %copy-start.7 = (f32[4096]{0:T(1024)S(1)}, f32[4096]{0:T(1024)}, u32[]{:S(2)}) copy-start(f32[4096]{0:T(1024)} %param.14) | copy-start | bytes 49156
  6.5 61.8 %all-gather.4.cloned.1.call-start = ((), (), s32[]{:S(2)}) async-start(), calls=%async_computation.1 | async-start | bytes 6291456 | tf_op jit(solution)/shard_map/all_gather | solution.py:61
  7.3 201.3 %all-gather.6.cloned.1.call-start = ((), (), s32[]{:S(2)}) async-start(), calls=%async_computation.2 | async-start | bytes 17825792 | tf_op jit(solution)/shard_map/all_gather | solution.py:104
  68.4 6.3 %copy-start.5 = (bf16[4096,512]{1,0:T(8,128)(2,1)S(1)}, bf16[4096,512]{1,0:T(8,128)(2,1)}, u32[]{:S(2)}) copy-start(bf16[4096,512]{1,0:T(8,128)(2,1)} %param.17) | copy-start | bytes 12582916
  68.4 6.3 %copy-start.6 = (bf16[512,4096]{1,0:T(8,128)(2,1)S(1)}, bf16[512,4096]{1,0:T(8,128)(2,1)}, u32[]{:S(2)}) copy-start(bf16[512,4096]{1,0:T(8,128)(2,1)} %all-gather.4.cloned.1.call-done) | copy-start | bytes 12582916
  74.7 4.0 copy-start.4
  78.4 497.9 %reduce-scatter.2.cloned.1.call-start = ((), (), s32[]{:S(2)}) async-start(), calls=%async_computation.3 | async-start | bytes 6291456 | tf_op jit(solution)/shard_map/reduce_scatter | solution.py:167
  226.4 1.7 copy-start
  231.3 1.3 copy-start.1
  234.4 1.7 copy-start.2
  239.3 1.3 copy-start.3
Sparse Core Ops, SparseCore 0:
  8.9 59.4 all-gather.3
  78.5 129.9 all-gather.5
  283.9 292.3 reduce-scatter.1
